TPU v7x, 32 devices: a whole 2x2x4 slice. The times are simulated.
32 devices in a mesh: dp: 8 (over y, x, core), vocab: 4 (over z).
Axes of the slice: x: 2, y: 2, z: 4, core: 2. Of those that a mesh axis runs over, the one named last changes fastest.
Arguments:
- resid: bfloat16 [2, 1024, 4096], P(None, 'dp'), may hold values from -6 to 6
- norm_gain: float32 [4096], replicated, may hold values from 0.5 to 1.5
- in_x: bfloat16 [4096, 4096], P('dp', 'vocab'), may hold values from -0.09375 to 0.09375
- in_z: bfloat16 [4096, 4096], P('dp', 'vocab'), may hold values from -0.09375 to 0.09375
- conv_w: float32 [4, 4096], P(None, 'vocab'), may hold values from -3 to 3
- conv_b: float32 [4096], P('vocab'), may hold values from -3 to 3
- xdt_w: bfloat16 [4096, 256], P('vocab'), may hold values from -0.09375 to 0.09375
- xbc_w: bfloat16 [4096, 32], P('vocab'), may hold values from -0.09375 to 0.09375
- dt_gain: float32 [256], replicated, may hold values from 0.5 to 1.5
- dt_proj: bfloat16 [256, 4096], P(None, 'vocab'), may hold values from -0.375 to 0.375
- dt_bias: float32 [4096], P('vocab'), may hold values from -4 to 1
- a_rate: float32 [4096, 16], P('vocab'), may hold values from 0.0001 to 1
- out_w: bfloat16 [4096, 4096], P('vocab'), may hold values from -0.09375 to 0.09375
- final_gain: float32 [4096], replicated, may hold values from 0.5 to 1.5
- head_w: bfloat16 [8192, 4096], P('vocab', 'dp'), as said below
- targets: int32 [2, 1024], P(None, 'dp'), may hold values from 0 to 8191
- lengths: int32 [2], replicated, may hold values from 256 to 1024
Outputs:
- hidden_out: bfloat16 [2, 1024, 4096], P(None, 'dp', 'vocab')
- token_logp: float32 [2, 1024], P(None, 'dp')
- mean_logp: float32 [], replicated
Inputs may be any that keep to these rules, and one draw needn't show every extreme that they name: `head_w`: entries lie within 720 / sqrt(4096) of zero.
All inputs are finite; a program needn't handle non-finite values.
Results may differ from a plain program's by a relative error of at most 0.019.
Values may be sent and summed in bfloat16 or wider, within the bound.
A program may use at most 128 MiB of HBM per device.

v0:
```python
import math

import jax
import jax.numpy as jnp
from jax import lax
from jax.sharding import PartitionSpec as P


def shifted(array, axis, by):
    peers = lax.axis_size(axis)
    pairs = [(i, i + by) for i in range(peers) if 0 <= i + by < peers]
    return lax.ppermute(array, axis, pairs)


def prefix(part, axis, combine, identity):
    place = lax.axis_index(axis)
    gathered = jax.tree.map(lambda a: lax.all_gather(a, axis), part)
    state = jax.tree.map(lambda a, e: jnp.zeros_like(a) + jnp.asarray(e, a.dtype), part, identity)

    def one(step, state):
        return combine(
            state, jax.tree.map(lambda a: lax.dynamic_index_in_dim(a, step, 0, False), gathered)
        )

    return lax.fori_loop(0, place, one, state)


def rms_norm(values, gain, epsilon):
    return values * lax.rsqrt(jnp.mean(values * values, axis=-1, keepdims=True) + epsilon) * gain


def head_logits(final, head_w):
    return lax.dot_general(
        final,
        lax.all_gather(head_w, "dp", axis=1, tiled=True),
        (((1,), (1,)), ((), ())),
        preferred_element_type=jnp.float32,
    )


def body(
    resid,
    norm_gain,
    in_x,
    in_z,
    conv_w,
    conv_b,
    xdt_w,
    xbc_w,
    dt_gain,
    dt_proj,
    dt_bias,
    a_rate,
    out_w,
    final_gain,
    head_w,
    targets,
    lengths,
):
    batch_count, local_len, width = resid.shape
    channels = in_x.shape[1]
    nstate = a_rate.shape[1]
    kernel_len = conv_w.shape[0]
    row_count = batch_count * local_len
    stream = resid.astype(jnp.float32)
    normed = rms_norm(stream, norm_gain, 1e-05).astype(jnp.bfloat16).reshape(row_count, width)
    x_acc = jnp.dot(
        normed, lax.all_gather(in_x, "dp", axis=0, tiled=True), preferred_element_type=jnp.float32
    )
    z_acc = jnp.dot(
        normed, lax.all_gather(in_z, "dp", axis=0, tiled=True), preferred_element_type=jnp.float32
    )
    x_inner = x_acc.astype(jnp.bfloat16).reshape(batch_count, local_len, channels)
    z_gate = z_acc.astype(jnp.bfloat16).reshape(batch_count, local_len, channels)
    before = shifted(x_inner[:, local_len - (kernel_len - 1) :, :], "dp", 1)
    padded = jnp.concatenate([before, x_inner], axis=1).astype(jnp.float32)
    conv_sum = jnp.zeros((batch_count, local_len, channels), jnp.float32) + conv_b
    for tap_index in range(kernel_len):
        conv_sum = conv_sum + conv_w[tap_index] * padded[:, tap_index : tap_index + local_len, :]
    conv_act = jax.nn.silu(conv_sum)
    conv_low = conv_act.astype(jnp.bfloat16).reshape(row_count, channels)
    dt_raw, bc_raw = (
        lax.psum(
            jnp.dot(conv_low, xdt_w, preferred_element_type=jnp.float32).astype(jnp.bfloat16),
            "vocab",
        ).astype(jnp.float32),
        lax.psum(
            jnp.dot(conv_low, xbc_w, preferred_element_type=jnp.float32).astype(jnp.bfloat16),
            "vocab",
        ).astype(jnp.float32),
    )
    dt_normed = rms_norm(dt_raw, dt_gain, 1e-06).astype(jnp.bfloat16)
    step_size = jax.nn.softplus(
        jnp.dot(dt_normed, dt_proj, preferred_element_type=jnp.float32) + dt_bias
    ).reshape(batch_count, local_len, channels)
    in_map = bc_raw[:, :nstate].reshape(batch_count, local_len, nstate)
    out_map = bc_raw[:, nstate:].reshape(batch_count, local_len, nstate)
    block_len = math.gcd(local_len, 16)
    block_count = local_len // block_len

    def by_block(values):
        return values.transpose(1, 0, 2).reshape(
            (block_count, block_len) + (values.shape[0], values.shape[2])
        )

    def run_block(carry_state, inputs):
        step_blk, conv_blk, in_blk, out_blk = inputs
        results = []
        for position in range(block_len):
            carry_state = (
                jnp.exp(-step_blk[position][..., None] * a_rate) * carry_state
                + (step_blk[position] * conv_blk[position])[..., None]
                * in_blk[position][:, None, :]
            )
            results.append(jnp.sum(carry_state * out_blk[position][:, None, :], axis=-1))
        return (carry_state, jnp.stack(results))

    start_state = jnp.zeros((batch_count, channels, nstate), jnp.float32)
    last_state, local_out = lax.scan(
        run_block,
        start_state,
        (by_block(step_size), by_block(conv_act), by_block(in_map), by_block(out_map)),
    )
    local_out = local_out.reshape(local_len, batch_count, channels).transpose(1, 0, 2)
    step_total = jnp.sum(step_size, axis=1)
    last_decay = jnp.exp(-step_total[..., None] * a_rate)

    def chain(earlier, later):
        return (earlier[0] * later[0], later[0] * earlier[1] + later[1])

    _, state_in = prefix(
        (last_decay, last_state),
        "dp",
        chain,
        (jnp.ones_like(last_decay), jnp.zeros_like(last_state)),
    )
    step_cumul = jnp.cumsum(step_size, axis=1)
    carried = jnp.sum(
        out_map[:, :, None, :] * jnp.exp(-step_cumul[..., None] * a_rate) * state_in[:, None, :, :],
        axis=-1,
    )
    mixed = local_out + carried
    gated = (
        (mixed * jax.nn.silu(z_gate.astype(jnp.float32)))
        .astype(jnp.bfloat16)
        .reshape(row_count, channels)
    )
    partial_value = jnp.dot(gated, out_w, preferred_element_type=jnp.float32)
    vocab_count = lax.axis_size("vocab")
    vocab_index = lax.axis_index("vocab")
    share_width = width // vocab_count
    flat_stream = stream.reshape(row_count, width)
    mixer_out = lax.psum(partial_value.astype(jnp.bfloat16), "vocab").astype(jnp.float32)
    hidden = (flat_stream + mixer_out).astype(jnp.bfloat16)
    final = rms_norm(hidden.astype(jnp.float32), final_gain, 1e-05).astype(jnp.bfloat16)
    hidden_share = lax.dynamic_slice_in_dim(hidden, vocab_index * share_width, share_width, 1)
    logits = head_logits(final, head_w)
    vocab_rows = head_w.shape[0]
    local_ids = targets.reshape(row_count) - vocab_index * vocab_rows
    entry_ids = lax.broadcasted_iota(jnp.int32, (row_count, vocab_rows), 1)
    picked = jnp.sum(jnp.where(entry_ids == local_ids[:, None], logits, 0.0), axis=-1)
    local_top = jnp.max(logits, axis=-1)
    global_top = lax.pmax(local_top, "vocab")
    exp_local = jnp.sum(jnp.exp(logits - global_top[:, None]), axis=-1)
    exp_total, picked_all = lax.psum((exp_local, picked), "vocab")
    log_total = global_top + jnp.log(exp_total)
    token_logp = (picked_all - log_total).reshape(batch_count, local_len)
    positions = lax.axis_index("dp") * local_len + jnp.arange(local_len, dtype=jnp.int32)
    valid_mask = positions[None, :] < lengths[:, None]
    masked_sum = jnp.sum(jnp.where(valid_mask, token_logp, 0.0))
    grand_sum = lax.psum(masked_sum, "dp")
    mean_logp = grand_sum / jnp.sum(lengths.astype(jnp.float32))
    return (hidden_share.reshape(batch_count, local_len, share_width), token_logp, mean_logp)


def solution(mesh):
    in_specs = (
        P(None, "dp", None),
        P(),
        P("dp", "vocab"),
        P("dp", "vocab"),
        P(None, "vocab"),
        P("vocab"),
        P("vocab", None),
        P("vocab", None),
        P(),
        P(None, "vocab"),
        P("vocab"),
        P("vocab", None),
        P("vocab", None),
        P(),
        P("vocab", "dp"),
        P(None, "dp"),
        P(),
    )
    out_specs = (P(None, "dp", "vocab"), P(None, "dp"), P())
    return jax.shard_map(body, mesh=mesh, in_specs=in_specs, out_specs=out_specs, check_vma=False)
```

profile of v0, /device:TPU:0, one launch (start us, length us, event | category | flops | bytes accessed | tf_op | source)
XLA Modules:
  0.0 477.5 jit_solution(16889401138438752080)
XLA Ops:
  8.0 2.1 multiply_reduce_fusion.17
  10.1 2.7 multiply_convert_fusion
  12.8 54.1 %all-gather.7.cloned.1.call-done = bf16[4096,1024]{1,0:T(8,128)(2,1)} async-done(((bf16[512,1024]{1,0:T(8,128)(2,1)}), bf16[4096,1024]{1,0:T(8,128)(2,1)}) %all-gather.7.cloned.1.call-update) | async-done | bytes 8388624 | tf_op jit(solution)/shard_map/all_gather | solution.py:68
  66.9 6.4 %convolution_convert_fusion.2 = bf16[256,1024]{1,0:T(8,128)(2,1)S(1)} fusion(bf16[256,4096]{1,0:T(8,128)(2,1)} %bitcast.279, bf16[4096,1024]{1,0:T(8,128)(2,1)} %all-gather.7.cloned.1.call-done), kind=kOutput, calls=%fused_computation.218 | convolution fusion | flops 2147745792 | bytes 11010048 | tf_op jit(solution)/shard_map/dot_general | solution.py:67
  73.3 2.3 collective-permute-start
  76.6 1.7 fusion.75
  80.3 18.7 %psum.43 = bf16[256,32]{0,1:T(8,128)(2,1)S(1)} all-reduce(bf16[256,32]{0,1:T(8,128)(2,1)S(1)} %convolution_convert_fusion.4), channel_id=1, replica_groups=mesh['dp'=8,'vocab'=4] {'vocab'}, use_global_device_ids=true, to_apply=%region_3.4 | all-reduce | flops 8192 | bytes 32768 | tf_op jit(solution)/shard_map/psum | solution.py:87
  99.4 17.4 %all-reduce.4.cloned.1.call-done = bf16[256,256]{1,0:T(8,128)(2,1)} async-done(((bf16[256,256]{1,0:T(8,128)(2,1)}), bf16[256,256]{1,0:T(8,128)(2,1)}) %all-reduce.4.cloned.1.call-update) | async-done | bytes 131088 | tf_op jit(solution)/shard_map/psum | solution.py:83
  117.8 1.8 bitcast_reduce_fusion
  120.5 1.9 copy.36
  122.4 48.8 %while.26 = (s32[]{:T(128)}, f32[2,1024,16]{1,2,0:T(8,128)S(1)}, f32[8,16,2,1024]{3,1,0,2:T(8,128)}, f32[8,16,2,1024]{3,2,1,0:T(2,128)}, f32[1024,16]{0,1:T(8,12...) while((s32[]{:T(128)}, f32[2,1024,16]{1,2,0:T(8,128)S(1)}, ...), condition=%wide.region_21.22_spmd.clone, body=%wide.region_4.21_spmd.clone.sunk | while | flops 4816914 | bytes 3422816 | solution.py:119
  122.4 1.6 constant_dynamic-slice_fusion.66
  128.5 1.6 constant_dynamic-slice_fusion.66
  134.6 1.6 constant_dynamic-slice_fusion.66
  140.7 1.6 constant_dynamic-slice_fusion.66
  146.7 1.6 constant_dynamic-slice_fusion.66
  158.8 1.9 constant_dynamic-slice_fusion.66
  165.2 1.6 constant_dynamic-slice_fusion.66
  172.7 6.3 %convolution_convert_fusion.1 = bf16[256,1024]{1,0:T(8,128)(2,1)S(1)} fusion(bf16[256,4096]{1,0:T(8,128)(2,1)} %bitcast.280, bf16[4096,1024]{1,0:T(8,128)(2,1)} %all-gather.11.cloned.1.call-done), kind=kOutput, calls=%fused_computation.217 | convolution fusion | flops 2147745792 | bytes 11010048 | tf_op jit(solution)/shard_map/dot_general | solution.py:70
  179.2 2.7 reduce_window_sum.11
  181.9 2.3 neg.205
  184.3 13.5 %all-gather.15.cloned.1.call-done = f32[16,1024,16]{1,2,0:T(8,128)} async-done(((f32[2,1024,16]{1,2,0:T(8,128)}), f32[16,1024,16]{1,2,0:T(8,128)}) %all-gather.15.cloned.1.call-update) | async-done | bytes 1048592 | tf_op jit(solution)/shard_map/all_gather | solution.py:17
  197.8 25.7 %all-gather.9.cloned.1.call-done = f32[8,2,1024,16]{2,3,1,0:T(8,128)} async-done(((f32[1,2,1024,16]{2,3,1,0:T(8,128)}), f32[8,2,1024,16]{2,3,1,0:T(8,128)}) %all-gather.9.cloned.1.call-update) | async-done | bytes 1048592 | tf_op jit(solution)/shard_map/all_gather | solution.py:17
  223.7 6.2 %multiply_reduce_fusion.16 = f32[2,128,1024]{2,1,0:T(8,128)S(1)} fusion(f32[2,1024,16]{1,2,0:T(8,128)S(1)} %get-tuple-element.92, f32[1024,16]{0,1:T(8,128)S(1)} %get-tuple-element.677, f32[2,128,1024]{2,1,0:T(8,128)} %neg.205, f32[2,128,16]{2,1,0:T(8,128)S(1)} %copy.41), kind=kLoop, calls=%fused_computation.196 | loop fusion | flops 16515072 | bytes 2310144 | tf_op jit(solution)/shard_map/reduce_sum | solution.py:138
  230.3 7.0 %convolution_convert_fusion = bf16[256,4096]{1,0:T(8,128)(2,1)} fusion(bf16[256,1024]{1,0:T(8,128)(2,1)S(1)} %bitcast.285, bf16[1024,4096]{1,0:T(8,128)(2,1)} %param.33), kind=kOutput, calls=%fused_computation.199 | convolution fusion | flops 2148532224 | bytes 11010048 | tf_op jit(solution)/shard_map/dot_general | solution.py:148
  238.8 92.2 %all-reduce.6.cloned.1.call-done = bf16[256,4096]{1,0:T(8,128)(2,1)} async-done(((bf16[256,4096]{1,0:T(8,128)(2,1)}), bf16[256,4096]{1,0:T(8,128)(2,1)}) %all-reduce.6.cloned.1.call-update) | async-done | bytes 2097168 | tf_op jit(solution)/shard_map/psum | solution.py:153
  331.0 2.5 fusion.49
  335.7 89.2 %all-gather.13.cloned.1.call-done = bf16[2048,4096]{1,0:T(8,128)(2,1)} async-done(((bf16[2048,512]{1,0:T(8,128)(2,1)}), bf16[2048,4096]{1,0:T(8,128)(2,1)}) %all-gather.13.cloned.1.call-update) | async-done | bytes 16777232 | tf_op jit(solution)/shard_map/all_gather | solution.py:35
  424.9 9.0 %fusion.78 = (f32[256]{0:T(256)S(1)}, f32[256,2048]{1,0:T(8,128)S(1)}) fusion(bf16[2048,4096]{1,0:T(8,128)(2,1)} %all-gather.13.cloned.1.call-done, bf16[256,4096]{1,0:T(8,128)(2,1)} %copy-done.6, f32[4096]{0:T(1024)S(1)} %copy-done.14, f32[256]{0:T(256)S(1)} %add_rsqrt_fusion), kind=kOutput, calls=%fused_computation.260 | convolution fusion | flops 4299685888 | bytes 20989952 | tf_op jit(solution)/shard_map/dot_general | solution.py:33
  433.9 11.7 %pmax.7 = f32[256]{0:T(256)S(1)} all-reduce(f32[256]{0:T(256)S(1)} %get-tuple-element.288), channel_id=1, replica_groups=mesh['dp'=8,'vocab'=4] {'vocab'}, use_global_device_ids=true, to_apply=%region_32.33 | all-reduce | flops 256 | bytes 2048 | tf_op jit(solution)/shard_map/pmax | solution.py:163
  446.2 8.4 %all-reduce = (f32[256]{0:T(256)S(1)}, f32[256]{0:T(256)S(1)}) all-reduce(f32[256]{0:T(256)S(1)} %get-tuple-element.144, f32[256]{0:T(256)S(1)} %get-tuple-element.143), channel_id=1, replica_groups=mesh['dp'=8,'vocab'=4] {'vocab'}, use_global_device_ids=true, to_apply=%region_30.31 | all-reduce | flops 512 | bytes 4096 | tf_op jit(solution)/shard_map/psum | solution.py:165
  455.8 12.4 %psum.47 = f32[]{:T(128)} all-reduce(f32[]{:T(128)} %get-tuple-element.284), channel_id=1, replica_groups=mesh['dp'=8,'vocab'=4] {'dp'}, use_global_device_ids=true, to_apply=%region_36.37 | all-reduce | flops 1 | bytes 8 | tf_op jit(solution)/shard_map/psum | solution.py:171
  (279 shorter events, 50.0 us)
Async XLA Ops:
  7.2 110.6 %copy-start = (bf16[256,1024]{1,0:T(8,128)(2,1)S(1)}, bf16[256,1024]{1,0:T(8,128)(2,1)}, u32[]{:S(2)}) copy-start(bf16[256,1024]{1,0:T(8,128)(2,1)} %param.30) | copy-start | bytes 1572868
  7.2 2.9 copy-start.3
  7.2 59.7 %all-gather.7.cloned.1.call-start = ((), (), s32[]{:S(2)}) async-start(), calls=%async_computation | async-start | bytes 9437184 | tf_op jit(solution)/shard_map/all_gather | solution.py:68
  7.9 108.8 %all-reduce.4.cloned.1.call-start = ((), (), s32[]{:S(2)}) async-start(), calls=%async_computation.1 | async-start | bytes 262144 | tf_op jit(solution)/shard_map/psum | solution.py:83
  66.9 8.7 %copy-start.10 = (f32[4,1024]{1,0:T(4,128)S(1)}, f32[4,1024]{1,0:T(4,128)}, u32[]{:S(2)}) copy-start(f32[4,1024]{1,0:T(4,128)} %param.25) | copy-start | bytes 49156
  66.9 9.7 %copy-start.11 = (f32[1024]{0:T(1024)S(1)}, f32[1024]{0:T(1024)}, u32[]{:S(2)}) copy-start(f32[1024]{0:T(1024)} %param.26) | copy-start | bytes 12292
  73.3 5.0 %copy-start.8 = (bf16[1024,256]{1,0:T(8,128)(2,1)S(1)}, bf16[1024,256]{1,0:T(8,128)(2,1)}, u32[]{:S(2)}) copy-start(bf16[1024,256]{1,0:T(8,128)(2,1)} %param.27) | copy-start | bytes 1572868
  73.3 3.1 collective-permute-start
  76.6 3.5 copy-start.9
  76.6 41.2 %copy-start.15 = (f32[1024]{0:T(1024)S(1)}, f32[1024]{0:T(1024)}, u32[]{:S(2)}) copy-start(f32[1024]{0:T(1024)} %param.31) | copy-start | bytes 12292
  76.6 41.2 %copy-start.16 = (f32[256]{0:T(256)S(1)}, f32[256]{0:T(256)}, u32[]{:S(2)}) copy-start(f32[256]{0:T(256)} %param.29) | copy-start | bytes 3076
  79.3 43.2 %copy-start.2 = (f32[1024,16]{0,1:T(8,128)S(1)}, f32[1024,16]{0,1:T(8,128)}, u32[]{:S(2)}) copy-start(f32[1024,16]{0,1:T(8,128)} %param.32) | copy-start | bytes 196612
  79.3 93.4 %all-gather.11.cloned.1.call-start = ((), (), s32[]{:S(2)}) async-start(), calls=%async_computation.3 | async-start | bytes 9437184 | tf_op jit(solution)/shard_map/all_gather | solution.py:71
  80.0 117.7 %all-gather.15.cloned.1.call-start = ((), (), s32[]{:S(2)}) async-start(), calls=%async_computation.6 | async-start | bytes 1179648 | tf_op jit(solution)/shard_map/all_gather | solution.py:17
  119.6 1.0 copy-start.5
  171.2 0.6 copy-start.4
  171.9 51.6 %all-gather.9.cloned.1.call-start = ((), (), s32[]{:S(2)}) async-start(), calls=%async_computation.2 | async-start | bytes 1179648 | tf_op jit(solution)/shard_map/all_gather | solution.py:17
  172.6 158.3 %all-reduce.6.cloned.1.call-start = ((), (), s32[]{:S(2)}) async-start(), calls=%async_computation.4 | async-start | bytes 4194304 | tf_op jit(solution)/shard_map/psum | solution.py:153
  223.7 6.3 %copy-start.7 = (f32[8,16,2,1024]{3,1,0,2:T(8,128)S(1)}, f32[8,16,2,1024]{3,1,0,2:T(8,128)}, u32[]{:S(2)}) copy-start(f32[8,16,2,1024]{3,1,0,2:T(8,128)} %get-tuple-element.90) | copy-start | bytes 3145732
  237.3 0.8 copy-start.13
  237.3 1.5 copy-start.12
  237.4 187.6 %all-gather.13.cloned.1.call-start = ((), (), s32[]{:S(2)}) async-start(), calls=%async_computation.5 | async-start | bytes 18874368 | tf_op jit(solution)/shard_map/all_gather | solution.py:35
  238.1 186.8 %copy-start.14 = (f32[4096]{0:T(1024)S(1)}, f32[4096]{0:T(1024)}, u32[]{:S(2)}) copy-start(f32[4096]{0:T(1024)} %param.34) | copy-start | bytes 49156
  333.5 1.4 copy-start.6
  424.9 44.6 %copy-start.1 = (bf16[256,1024]{1,0:T(8,128)(2,1)S(1)}, bf16[256,1024]{1,0:T(8,128)(2,1)}, u32[]{:S(2)}) copy-start(bf16[256,1024]{1,0:T(8,128)(2,1)} %param.30) | copy-start | bytes 1572868
Sparse Core Ops, SparseCore 0:
  9.9 56.9 all-gather.6
  79.4 37.2 all-reduce.3
  118.6 53.9 all-gather.10
  174.4 23.3 all-gather.14
  200.1 23.3 all-gather.8
  237.5 93.4 all-reduce.5
  332.8 92.0 all-gather.12
where the time goes:
time: 480 us; the launch traced here: 478 us
  waiting for transfers between devices  295 us (61%)
  other arithmetic  51.9 us (11%)
  blocking collectives  51.3 us (11%)
  matrix products  31.7 us (7%)
  local copies, waits for them, and re-layouts  27.4 us (6%)
  between operations  16.9 us (4%)
    psum x1, waiting for transfers between devices, body(): lax.psum(partial_value.astype(jnp.bfloat16), 'vocab').astype(jnp.float32)  92.2 us
    all_gather x1, waiting for transfers between devices, head_logits(): lax.all_gather(head_w, 'dp', axis=1, tiled=True)  89.2 us
    all_gather x1, waiting for transfers between devices, body(): lax.all_gather(in_x, 'dp', axis=0, tiled=True)  54.1 us
    all_gather x2, waiting for transfers between devices, prefix(): gathered = jax.tree.map(lambda a: lax.all_gather(a, axis), part)  39.2 us
    psum x1, blocking collectives, body(): lax.psum(jnp.dot(conv_low, xbc_w, preferred_element_type=jnp.float32).ast...  18.7 us
    psum x1, waiting for transfers between devices, body(): lax.psum(jnp.dot(conv_low, xdt_w, preferred_element_type=jnp.float32).ast...  17.4 us
    neg x16, other arithmetic, run_block(): -step_blk[position][..., None] * a_rate  14.9 us
    slice x8, local copies, waits for them, and re-layouts, run_block(): conv_blk[position]  13.3 us
  transfers between devices with their start and end apart: 8, of which 7 were waited for; matrix products, arithmetic and copies ran while one was open for 16% of the time, Pallas kernels for 0%

commit v1 on v0

v1 whole, which is shorter than its diff:
```python
import functools

import jax
import jax.numpy as jnp
from jax import lax
from jax.experimental import pallas as pl
from jax.experimental.pallas import tpu as pltpu
from jax.sharding import PartitionSpec as P

MESH = pl.DeviceIdType.MESH
VMEM = pl.BlockSpec(memory_space=pltpu.VMEM)
CHUNKS = 8
LANE = 128


def peer(axis, shift):
    size = lax.axis_size(axis)
    return {axis: lax.rem(lax.axis_index(axis) + shift, size)}


def greet(axes):
    barrier = pltpu.get_barrier_semaphore()
    count = 0
    for axis in axes:
        for shift in range(1, lax.axis_size(axis)):
            pl.semaphore_signal(barrier, inc=1, device_id=peer(axis, shift), device_id_type=MESH)
            count += 1
    pl.semaphore_wait(barrier, count)


def remote(src, dst, send_sem, recv_sem, device):
    return pltpu.make_async_remote_copy(
        src_ref=src, dst_ref=dst, send_sem=send_sem, recv_sem=recv_sem,
        device_id=device, device_id_type=MESH,
    )


def call(kernel, out_shape, scratch, cid, cost_us, name):
    return pl.pallas_call(
        kernel,
        out_shape=out_shape,
        scratch_shapes=scratch,
        compiler_params=pltpu.CompilerParams(
            collective_id=cid, has_side_effects=True, vmem_limit_bytes=56 * 1024 * 1024
        ),
        cost_estimate=pl.CostEstimate(
            flops=0, bytes_accessed=int(cost_us * 3.0e6), transcendentals=0
        ),
        name=name,
    )


def dt_kernel(nv, ranks, part_ref, gain_ref, out_ref, recv, mine, s1, r1, s2, r2):
    me = lax.axis_index("vocab")
    rows = part_ref.shape[0] // nv
    greet(("vocab",))
    copies = []
    for shift in range(1, nv):
        target = lax.rem(me + shift, nv)
        copy = remote(
            part_ref.at[pl.ds(pl.multiple_of(target * rows, rows), rows)], recv.at[shift - 1],
            s1.at[shift - 1], r1.at[shift - 1], peer("vocab", shift),
        )
        copy.start()
        copies.append(copy)
    own = pl.ds(pl.multiple_of(me * rows, rows), rows)
    total = part_ref[own, :].astype(jnp.float32)
    for shift in range(1, nv):
        copies[shift - 1].wait()
        total = total + recv[shift - 1].astype(jnp.float32)
    dt = total[:, :ranks]
    scale = lax.rsqrt(jnp.mean(dt * dt, axis=-1, keepdims=True) + 1e-06)
    mine[:, :ranks] = (dt * scale * gain_ref[...]).astype(jnp.bfloat16)
    mine[:, ranks:] = total[:, ranks:].astype(jnp.bfloat16)
    copies = []
    for shift in range(1, nv):
        copy = remote(
            mine, out_ref.at[own], s2.at[shift - 1], r2.at[shift - 1], peer("vocab", shift)
        )
        copy.start()
        copies.append(copy)
    out_ref[own, :] = mine[...]
    for copy in copies:
        copy.wait()


def dt_reduce(part, gain, nv, ranks):
    rows, cols = part.shape
    sems = [pltpu.SemaphoreType.DMA((nv - 1,))] * 4
    return call(
        functools.partial(dt_kernel, nv, ranks),
        jax.ShapeDtypeStruct((rows, cols), jnp.bfloat16),
        [
            pltpu.VMEM((nv - 1, rows // nv, cols), jnp.bfloat16),
            pltpu.VMEM((rows // nv, cols), jnp.bfloat16),
        ] + sems,
        1, 10, "dt_reduce",
    )(part, gain)


def scan_kernel(
    nd, batch, nstate, ranks, low_ref, proj_ref, bias_ref, conv_ref, rate_ref, out_ref,
    step, drive, maps, result, state, sums, agg, tot, agg_in, tot_in, s1, r1, s2, r2,
):
    me = lax.axis_index("dp")
    rows, chans = conv_ref.shape
    lanes = chans // LANE
    length = rows // batch
    span = length // CHUNKS
    greet(("dp",))
    low_dt = low_ref[:, :ranks]
    maps[...] = low_ref[:, ranks:].astype(jnp.float32)
    wide = 2 if lanes % 2 == 0 else 1
    size = wide * LANE

    @pl.loop(0, lanes // wide)
    def _(g):
        cols = pl.ds(pl.multiple_of(g * size, size), size)
        raw = jnp.dot(
            low_dt, proj_ref[:, cols], preferred_element_type=jnp.float32
        ) + bias_ref[:, cols]
        value = jnp.maximum(raw, 0.0) + jnp.log1p(jnp.exp(-jnp.abs(raw)))
        pushed = value * conv_ref[:, cols]
        for w in range(wide):
            k = g * wide + w
            step[k] = value[:, w * LANE : (w + 1) * LANE]
            drive[k] = pushed[:, w * LANE : (w + 1) * LANE]

    def run(with_out):
        @pl.loop(0, lanes // wide)
        def _(g):
            for b in range(batch):
                rates = [
                    [
                        rate_ref[pl.ds(n, 1), pl.ds(pl.multiple_of((g * wide + w) * LANE, LANE), LANE)]
                        for n in range(nstate)
                    ]
                    for w in range(wide)
                ]

                def one(t, carry):
                    at = pl.ds(b * length + t, CHUNKS, stride=span)
                    both = maps[at, :]
                    held, extra = carry
                    held, extra = list(held), list(extra)
                    now = [step[g * wide + w, at, :] for w in range(wide)]
                    push = [drive[g * wide + w, at, :] for w in range(wide)]
                    acc = [None] * wide
                    for n in range(nstate):
                        into = jnp.broadcast_to(both[:, n : n + 1], (CHUNKS, LANE))
                        if with_out:
                            outof = jnp.broadcast_to(
                                both[:, nstate + n : nstate + n + 1], (CHUNKS, LANE)
                            )
                        for w in range(wide):
                            i = w * nstate + n
                            held[i] = (
                                jnp.exp(-now[w] * rates[w][n]) * held[i] + push[w] * into
                            )
                            if with_out:
                                term = held[i] * outof
                                acc[w] = term if acc[w] is None else acc[w] + term
                    for w in range(wide):
                        if with_out:
                            result[g * wide + w, at, :] = acc[w]
                        else:
                            extra[w] = extra[w] + now[w]
                    return tuple(held), tuple(extra)

                zero = jnp.zeros((CHUNKS, LANE), jnp.float32)
                if with_out:
                    first = tuple(
                        state[b, g * wide + w, pl.ds(n * CHUNKS, CHUNKS), :]
                        for w in range(wide) for n in range(nstate)
                    )
                    lax.fori_loop(0, span, one, (first, ()))
                else:
                    held, extra = lax.fori_loop(
                        0, span, one, ((zero,) * (wide * nstate), (zero,) * wide)
                    )
                    for w in range(wide):
                        for n in range(nstate):
                            state[b, g * wide + w, pl.ds(n * CHUNKS, CHUNKS), :] = held[
                                w * nstate + n
                            ]
                        sums[b, g * wide + w] = extra[w]

    run(False)

    @pl.loop(0, lanes)
    def _(k):
        cols = pl.ds(pl.multiple_of(k * LANE, LANE), LANE)
        rate = rate_ref[:, cols]
        for b in range(batch):
            carry = jnp.zeros((nstate, LANE), jnp.float32)
            for c in range(CHUNKS):
                part = state[b, k, pl.ds(c, nstate, stride=CHUNKS), :]
                carry = jnp.exp(-sums[b, k, pl.ds(c, 1), :] * rate) * carry + part
            agg[pl.ds(b * nstate, nstate), cols] = carry.astype(jnp.bfloat16)
            tot[pl.ds(b, 1), cols] = jnp.sum(sums[b, k], axis=0, keepdims=True)

    def pair(source, target):
        device = {"dp": target}
        return (
            remote(agg, agg_in.at[source], s1.at[target], r1.at[source], device),
            remote(tot, tot_in.at[source], s2.at[target], r2.at[source], device),
        )

    for other in range(nd):
        @pl.when(other > me)
        def _():
            for copy in pair(me, other):
                copy.start()

    for other in range(nd):
        @pl.when(other < me)
        def _():
            for copy in pair(other, me):
                copy.wait_recv()

    @pl.loop(0, lanes)
    def _(k):
        cols = pl.ds(pl.multiple_of(k * LANE, LANE), LANE)
        rate = rate_ref[:, cols]
        for b in range(batch):
            def earlier(d, carry):
                decay = jnp.exp(-tot_in[d, pl.ds(b, 1), cols] * rate)
                return decay * carry + agg_in[d, pl.ds(b * nstate, nstate), cols].astype(
                    jnp.float32
                )

            carry = lax.fori_loop(0, me, earlier, jnp.zeros((nstate, LANE), jnp.float32))
            for c in range(CHUNKS):
                at = pl.ds(c, nstate, stride=CHUNKS)
                part = state[b, k, at, :]
                state[b, k, at, :] = carry
                carry = jnp.exp(-sums[b, k, pl.ds(c, 1), :] * rate) * carry + part

    run(True)

    @pl.loop(0, lanes)
    def _(k):
        out_ref[:, pl.ds(pl.multiple_of(k * LANE, LANE), LANE)] = result[k]

    for other in range(nd):
        @pl.when(other > me)
        def _():
            for copy in pair(me, other):
                copy.wait_send()


def scan(low, proj, bias, conv, rate, batch, nd, ranks):
    rows, chans = conv.shape
    nstate = rate.shape[0]
    lanes = chans // LANE
    big = pltpu.VMEM((lanes, rows, LANE), jnp.float32)
    return call(
        functools.partial(scan_kernel, nd, batch, nstate, ranks),
        jax.ShapeDtypeStruct((rows, chans), jnp.float32),
        [
            big, big,
            pltpu.VMEM((rows, low.shape[1] - ranks), jnp.float32),
            big,
            pltpu.VMEM((batch, lanes, nstate * CHUNKS, LANE), jnp.float32),
            pltpu.VMEM((batch, lanes, CHUNKS, LANE), jnp.float32),
            pltpu.VMEM((batch * nstate, chans), jnp.bfloat16),
            pltpu.VMEM((batch, chans), jnp.float32),
            pltpu.VMEM((nd, batch * nstate, chans), jnp.bfloat16),
            pltpu.VMEM((nd, batch, chans), jnp.float32),
        ] + [pltpu.SemaphoreType.DMA((nd,))] * 4,
        2, 30, "scan",
    )(low, proj, bias, conv, rate)


def out_kernel(nv, gated_ref, w_ref, resid_ref, out_ref, sent, recv, mine, s1, r1, s2, r2):
    me = lax.axis_index("vocab")
    rows, width = resid_ref.shape
    share = width // nv
    greet(("vocab",))

    def columns(index):
        return pl.ds(pl.multiple_of(index * share, share), share)

    tile = min(512, share)

    def product(index, put):
        @pl.loop(0, share // tile)
        def _(k):
            at = pl.multiple_of(index * share + k * tile, tile)
            put(
                pl.ds(pl.multiple_of(k * tile, tile), tile), pl.ds(at, tile),
                jnp.dot(
                    gated_ref[...], w_ref[:, pl.ds(at, tile)], preferred_element_type=jnp.float32
                ),
            )

    copies = {}
    order = sorted(range(1, nv), key=lambda s: abs(s - nv / 2))
    for shift in order:
        def put(local, whole, value):
            sent[shift - 1, :, local] = value.astype(jnp.bfloat16)

        product(lax.rem(me + shift, nv), put)
        copy = remote(
            sent.at[shift - 1], recv.at[shift - 1],
            s1.at[shift - 1], r1.at[shift - 1], peer("vocab", shift),
        )
        copy.start()
        copies[shift] = copy

    def put(local, whole, value):
        mine[:, local] = value

    product(me, put)
    for shift in order:
        copies[shift].wait()

    @pl.loop(0, share // tile)
    def _(k):
        local = pl.ds(pl.multiple_of(k * tile, tile), tile)
        whole = pl.ds(pl.multiple_of(me * share + k * tile, tile), tile)
        total = mine[:, local]
        for shift in range(1, nv):
            total = total + recv[shift - 1, :, local].astype(jnp.float32)
        hidden = (resid_ref[:, whole].astype(jnp.float32) + total).astype(jnp.bfloat16)
        sent[nv - 1, :, local] = hidden
        out_ref[:, whole] = hidden

    copies = []
    for shift in range(1, nv):
        copy = remote(
            sent.at[nv - 1], out_ref.at[:, columns(me)],
            s2.at[shift - 1], r2.at[shift - 1], peer("vocab", shift),
        )
        copy.start()
        copies.append(copy)
    for copy in copies:
        copy.wait()


def out_reduce(gated, w, resid, nv):
    rows, width = resid.shape
    share = width // nv
    sems = [pltpu.SemaphoreType.DMA((nv - 1,))] * 4
    return call(
        functools.partial(out_kernel, nv),
        jax.ShapeDtypeStruct((rows, width), jnp.bfloat16),
        [
            pltpu.VMEM((nv, rows, share), jnp.bfloat16),
            pltpu.VMEM((nv - 1, rows, share), jnp.bfloat16),
            pltpu.VMEM((rows, share), jnp.float32),
        ] + sems,
        3, 60, "out_reduce",
    )(gated, w, resid)


def tail_kernel(nv, nd, stats_ref, mask_ref, logp_ref, sum_ref, recv, part, parts, s1, r1, s2, r2):
    greet(("vocab", "dp"))
    copies = []
    for shift in range(1, nv):
        copy = remote(
            stats_ref, recv.at[shift - 1], s1.at[shift - 1], r1.at[shift - 1],
            peer("vocab", shift),
        )
        copy.start()
        copies.append(copy)
    for copy in copies:
        copy.wait()
    everyone = [stats_ref[...]] + [recv[k] for k in range(nv - 1)]
    top = everyone[0][0:1]
    for stats in everyone[1:]:
        top = jnp.maximum(top, stats[0:1])
    total = jnp.zeros_like(top)
    picked = jnp.zeros_like(top)
    for stats in everyone:
        total = total + stats[1:2] * jnp.exp(stats[0:1] - top)
        picked = picked + stats[2:3]
    logp = picked - (top + jnp.log(total))
    logp_ref[...] = logp
    masked = jnp.sum(jnp.where(mask_ref[...] > 0.0, logp, 0.0), axis=-1, keepdims=True)
    part[...] = jnp.broadcast_to(masked, part.shape)
    copies = []
    for shift in range(1, nd):
        copy = remote(
            part, parts.at[shift - 1], s2.at[shift - 1], r2.at[shift - 1], peer("dp", shift)
        )
        copy.start()
        copies.append(copy)
    grand = part[...]
    for shift in range(1, nd):
        copies[shift - 1].wait()
        grand = grand + parts[shift - 1]
    sum_ref[...] = grand


def tail(stats, mask, nv, nd):
    rows = stats.shape[1]
    return call(
        functools.partial(tail_kernel, nv, nd),
        (
            jax.ShapeDtypeStruct((1, rows), jnp.float32),
            jax.ShapeDtypeStruct((8, 128), jnp.float32),
        ),
        [
            pltpu.VMEM((nv - 1, 8, rows), jnp.float32),
            pltpu.VMEM((8, 128), jnp.float32),
            pltpu.VMEM((nd - 1, 8, 128), jnp.float32),
        ] + [pltpu.SemaphoreType.DMA((nv - 1,))] * 2 + [pltpu.SemaphoreType.DMA((nd - 1,))] * 2,
        4, 6, "tail",
    )(stats, mask)


def rms_norm(values, gain, epsilon):
    return values * lax.rsqrt(jnp.mean(values * values, axis=-1, keepdims=True) + epsilon) * gain


def body(
    resid, norm_gain, in_x, in_z, conv_w, conv_b, xdt_w, xbc_w, dt_gain, dt_proj, dt_bias,
    a_rate, out_w, final_gain, head_w, targets, lengths,
):
    nv, nd = lax.axis_size("vocab"), lax.axis_size("dp")
    batch, local_len, width = resid.shape
    channels = in_x.shape[1]
    nstate = a_rate.shape[1]
    ranks = xdt_w.shape[1]
    kernel_len = conv_w.shape[0]
    rows = batch * local_len
    vocab_index = lax.axis_index("vocab")

    full_x = lax.all_gather(in_x, "dp", axis=0, tiled=True)
    in_z, _ = lax.optimization_barrier((in_z, in_x))
    full_z = lax.all_gather(in_z, "dp", axis=0, tiled=True)
    full_head = lax.all_gather(head_w, "dp", axis=1, tiled=True)

    pad = -(2 * nstate) % 128
    low_w = jnp.concatenate([xdt_w, xbc_w, jnp.zeros((channels, pad), jnp.bfloat16)], axis=1)
    flat = resid.reshape(rows, width)
    stream = flat.astype(jnp.float32)
    normed = rms_norm(stream, norm_gain, 1e-05).astype(jnp.bfloat16)
    x_inner = (
        jnp.dot(normed, full_x, preferred_element_type=jnp.float32)
        .astype(jnp.bfloat16)
        .reshape(batch, local_len, channels)
    )
    before = lax.ppermute(
        x_inner[:, local_len - (kernel_len - 1) :, :], "dp", [(i, i + 1) for i in range(nd - 1)]
    )
    padded = jnp.concatenate([before, x_inner], axis=1).astype(jnp.float32)
    conv_sum = jnp.zeros((batch, local_len, channels), jnp.float32) + conv_b
    for tap in range(kernel_len):
        conv_sum = conv_sum + conv_w[tap] * padded[:, tap : tap + local_len, :]
    conv_act = jax.nn.silu(conv_sum).reshape(rows, channels)
    part = jnp.dot(
        conv_act.astype(jnp.bfloat16), low_w, preferred_element_type=jnp.float32
    ).astype(jnp.bfloat16)
    low = dt_reduce(part, dt_gain[None, :], nv, ranks)
    mixed = scan(low, dt_proj, dt_bias[None, :], conv_act, a_rate.T, batch, nd, ranks)
    z_gate = (
        jnp.dot(normed, full_z, preferred_element_type=jnp.float32)
        .astype(jnp.bfloat16)
        .astype(jnp.float32)
    )
    gated = (mixed * jax.nn.silu(z_gate)).astype(jnp.bfloat16)
    hidden = out_reduce(gated, out_w, flat, nv)
    share = width // nv
    hidden_share = lax.dynamic_slice_in_dim(hidden, vocab_index * share, share, 1)
    final = rms_norm(hidden.astype(jnp.float32), final_gain, 1e-05).astype(jnp.bfloat16)
    logits = lax.dot_general(
        final, full_head, (((1,), (1,)), ((), ())), preferred_element_type=jnp.float32
    )
    vocab_rows = head_w.shape[0]
    local_ids = targets.reshape(rows) - vocab_index * vocab_rows
    entry_ids = lax.broadcasted_iota(jnp.int32, (rows, vocab_rows), 1)
    picked = jnp.sum(jnp.where(entry_ids == local_ids[:, None], logits, 0.0), axis=-1)
    top = jnp.max(logits, axis=-1)
    total = jnp.sum(jnp.exp(logits - top[:, None]), axis=-1)
    stats = jnp.concatenate(
        [top[None], total[None], picked[None], jnp.zeros((5, rows), jnp.float32)], axis=0
    )
    positions = lax.axis_index("dp") * local_len + jnp.arange(local_len, dtype=jnp.int32)
    mask = (positions[None, :] < lengths[:, None]).astype(jnp.float32).reshape(1, rows)
    logp, grand = tail(stats, mask, nv, nd)
    mean_logp = grand[0, 0] / jnp.sum(lengths.astype(jnp.float32))
    return (
        hidden_share.reshape(batch, local_len, share),
        logp.reshape(batch, local_len),
        mean_logp,
    )


def solution(mesh):
    in_specs = (
        P(None, "dp", None), P(), P("dp", "vocab"), P("dp", "vocab"), P(None, "vocab"), P("vocab"),
        P("vocab", None), P("vocab", None), P(), P(None, "vocab"), P("vocab"), P("vocab", None),
        P("vocab", None), P(), P("vocab", "dp"), P(None, "dp"), P(),
    )
    out_specs = (P(None, "dp", "vocab"), P(None, "dp"), P())
    return jax.shard_map(body, mesh=mesh, in_specs=in_specs, out_specs=out_specs, check_vma=False)
```

time: 480 us -> 294 us (0.61)
  waiting for transfers between devices: 295 us -> 58.3 us
  Pallas kernels: 0 us -> 180 us
  blocking collectives: 51.3 us -> 0 us
  other arithmetic: 51.9 us -> 7.55 us
  local copies, waits for them, and re-layouts: 27.4 us -> 5.26 us
  matrix products: 31.7 us -> 23.5 us
    pallas_call x0 -> x4, Pallas kernels: none -> 180 us  [the longest x1 102 us: out_reduce(): call(functools.partial(out_kernel, nv), jax.ShapeDtypeStruct((rows, width...]
    all_gather x5 -> x3, waiting for transfers between devices: 183 us -> 56.3 us  [the longest x1 56.2 us: body(): full_x = lax.all_gather(in_x, 'dp', axis=0, tiled=True)]
    psum x2 -> x0, waiting for transfers between devices: 110 us -> none  [the longest x1 92.2 us: body(): lax.psum(partial_value.astype(jnp.bfloat16), 'vocab').astype(jnp.float32)]
    psum x3 -> x0, blocking collectives: 39.6 us -> none  [the longest x1 18.7 us: body(): lax.psum(jnp.dot(conv_low, xbc_w, preferred_element_type=jnp.float32).ast...]
    reduce_sum x44 -> x2, other arithmetic: 20.6 us -> 2.83 us  [the longest x1 2.21 us: body(): total = jnp.sum(jnp.exp(logits - top[:, None]), axis=-1)]
    neg x18 -> x0, other arithmetic: 17.3 us -> none  [the longest x16 14.9 us: run_block(): -step_blk[position][..., None] * a_rate]
    slice x11 -> x3, local copies, waits for them, and re-layouts: 13.3 us -> 1.22 us  [the longest x1 1.2 us: body(): mean_logp = grand[0, 0] / jnp.sum(lengths.astype(jnp.float32))]
    pmax x1 -> x0, blocking collectives: 11.7 us -> none  [body(): global_top = lax.pmax(local_top, 'vocab')]
  transfers between devices with their start and end apart: 8 -> 4, of which waited for: 7 -> 1; matrix products, arithmetic and copies ran while one was open for 16% -> 7% of each run, Pallas kernels for 0% -> 53%
where the time goes in v1:
time: 294 us
  Pallas kernels  180 us (61%)
  waiting for transfers between devices  58.3 us (20%)
  matrix products  23.5 us (8%)
  between operations  16.4 us (6%)
  other arithmetic  7.55 us (3%)
  local copies, waits for them, and re-layouts  5.26 us (2%)
    pallas_call x1, Pallas kernels, out_reduce(): call(functools.partial(out_kernel, nv), jax.ShapeDtypeStruct((rows, width...  102 us
    all_gather x1, waiting for transfers between devices, body(): full_x = lax.all_gather(in_x, 'dp', axis=0, tiled=True)  56.2 us
    pallas_call x1, Pallas kernels, scan(): call(functools.partial(scan_kernel, nd, batch, nstate, ranks), jax.ShapeD...  39 us
    pallas_call x1, Pallas kernels, tail(): call(functools.partial(tail_kernel, nv, nd), (jax.ShapeDtypeStruct((1, ro...  23.2 us
    pallas_call x1, Pallas kernels, dt_reduce(): call(functools.partial(dt_kernel, nv, ranks), jax.ShapeDtypeStruct((rows,...  16.2 us
    dot_general x1, matrix products, body(): lax.dot_general(final, full_head, (((1,), (1,)), ((), ())), preferred_ele...  9.69 us
    dot_general x1, matrix products, body(): jnp.dot(normed, full_z, preferred_element_type=jnp.float32)  6.91 us
  transfers between devices with their start and end apart: 4, of which 1 were waited for; matrix products, arithmetic and copies ran while one was open for 7% of the time, Pallas kernels for 53%

profile of v1, /device:TPU:0, one launch (start us, length us, event | category | flops | bytes accessed | tf_op | source)
XLA Modules:
  0.0 293.9 jit_solution(10398252869500459722)
XLA Ops:
  7.2 0.0 all-gather.4.cloned.1.call-start
  7.2 0.7 all-gather.4.cloned.1.call-update
  7.9 0.0 all-gather.6.cloned.1.call-start
  8.0 0.7 all-gather.6.cloned.1.call-update
  8.7 0.0 all-gather.8.cloned.1.call-start
  8.7 0.7 all-gather.8.cloned.1.call-update
  9.5 0.5 multiply_reduce_fusion
  10.0 0.6 compare_convert_fusion
  10.7 56.2 %all-gather.4.cloned.1.call-done = bf16[4096,1024]{1,0:T(8,128)(2,1)} async-done(((bf16[512,1024]{1,0:T(8,128)(2,1)}), bf16[4096,1024]{1,0:T(8,128)(2,1)}) %all-gather.4.cloned.1.call-update) | async-done | bytes 8388624 | tf_op jit(solution)/shard_map/all_gather | solution.py:430
  66.9 5.8 %convolution_convert_fusion.1 = bf16[256,1024]{1,0:T(8,128)(2,1)S(1)} fusion(bf16[4096,1024]{1,0:T(8,128)(2,1)} %all-gather.4.cloned.1.call-done, bf16[256,4096]{1,0:T(8,128)(2,1)S(1)} %bitcast.25, f32[4096]{0:T(1024)S(1)} %copy-done.9, f32[256]{0:T(256)S(1)} %rsqrt_bitcast_fusion), kind=kOutput, calls=%fused_computation.16 | convolution fusion | flops 2151940096 | bytes 11027456 | tf_op jit(solution)/shard_map/dot_general | solution.py:441
  72.7 2.3 collective-permute-start
  75.1 0.6 convert_reduce_fusion
  75.7 0.2 copy.20
  75.9 0.1 pad.6.clone
  75.9 0.1 pad.3.clone
  76.0 0.1 maximum_convert_fusion
  76.2 0.7 divide_multiply_fusion
  76.9 0.4 copy-done.8
  77.3 1.1 convolution_convert_fusion.2.part_ref
  78.4 16.2 %dt_reduce.1.low_ref = bf16[256,384]{1,0:T(8,128)(2,1)} custom-call(bf16[256,384]{1,0:T(8,128)(2,1)} %convolution_convert_fusion.2.part_ref, f32[1,256]{1,0:T(1,128)} %bitcast.42), custom_call_target="tpu_custom_call" | custom-call | bytes 30000000 | tf_op jit(solution)/shard_map/dt_reduce/pallas_call | solution.py:90
  94.7 39.0 %scan.1 = f32[256,1024]{1,0:T(8,128)} custom-call(bf16[256,384]{1,0:T(8,128)(2,1)} %dt_reduce.1.low_ref, bf16[256,1024]{1,0:T(8,128)(2,1)} %proj_ref.1, f32[1,1024]{1,0:T(1,128)} %bitcast.37, f32[256,1024]{1,0:T(8,128)} %bitcast.28, f32[16,1024]{1,0:T(8,128)} %bitcast.32), custom_call_target="tpu_custom_call" | custom-call | bytes 90000000 | tf_op jit(solution)/shard_map/scan/pallas_call | solution.py:257
  133.7 0.0 all-gather.6.cloned.1.call-done
  133.7 6.9 %fusion.11.gated_ref = bf16[256,1024]{1,0:T(8,128)(2,1)} fusion(f32[256,1024]{1,0:T(8,128)} %scan.1, bf16[4096,1024]{1,0:T(8,128)(2,1)} %all-gather.6.cloned.1.call-done, bf16[256,4096]{1,0:T(8,128)(2,1)S(1)} %bitcast.26, f32[4096]{0:T(1024)S(1)} %copy-done.9, f32[256]{0:T(256)S(1)} %rsqrt_bitcast_fusion), kind=kOutput, calls=%fused_computation.22 | convolution fusion | flops 2153775104 | bytes 12076032 | tf_op jit(solution)/shard_map/dot_general | solution.py:459
  140.6 101.9 %out_reduce.1 = bf16[256,4096]{1,0:T(8,128)(2,1)} custom-call(bf16[256,1024]{1,0:T(8,128)(2,1)} %fusion.11.gated_ref, bf16[1024,4096]{1,0:T(8,128)(2,1)} %w_ref.1, bf16[256,4096]{1,0:T(8,128)(2,1)} %bitcast.24), custom_call_target="tpu_custom_call" | custom-call | bytes 180000000 | tf_op jit(solution)/shard_map/out_reduce/pallas_call | solution.py:345
  242.5 2.0 constant_dynamic-slice_fusion
  244.6 2.1 fusion
  246.7 9.7 %fusion.24 = (f32[256]{0:T(256)S(1)}, f32[256,2048]{1,0:T(8,128)}) fusion(bf16[2048,4096]{1,0:T(8,128)(2,1)} %all-gather.8.cloned.1.call-done, bf16[256,4096]{1,0:T(8,128)(2,1)S(1)} %copy-done, f32[4096]{0:T(1024)S(1)} %copy-done.10, f32[256]{0:T(256)S(1)} %add_rsqrt_fusion), kind=kOutput, calls=%fused_computation.49 | convolution fusion | flops 4299685888 | bytes 20989952 | tf_op jit(solution)/shard_map/dot_general | solution.py:468
  256.4 2.2 exponential_reduce_fusion
  258.6 0.7 maximum_maximum_fusion.stats_ref
  259.3 23.2 %tail.1 = (f32[1,256]{1,0:T(1,128)}, f32[8,128]{1,0:T(8,128)}) custom-call(f32[8,256]{1,0:T(8,128)} %maximum_maximum_fusion.stats_ref, f32[1,256]{1,0:T(1,128)} %bitcast.41), custom_call_target="tpu_custom_call" | custom-call | bytes 18000000 | tf_op jit(solution)/shard_map/tail/pallas_call | solution.py:398
  282.5 1.2 slice.39
  285.0 1.2 copy.22
  (31 shorter events, 0.1 us)
Async XLA Ops:
  7.2 2.3 copy-start.1
  7.2 59.7 %all-gather.4.cloned.1.call-start = ((), (), s32[]{:S(2)}) async-start(), calls=%async_computation | async-start | bytes 9437184 | tf_op jit(solution)/shard_map/all_gather | solution.py:430
  7.9 125.8 %all-gather.6.cloned.1.call-start = ((), (), s32[]{:S(2)}) async-start(), calls=%async_computation.1 | async-start | bytes 9437184 | tf_op jit(solution)/shard_map/all_gather | solution.py:432
  8.7 1.3 copy-start.6
  8.7 1.3 copy-start.7
  8.7 2.0 copy-start.4
  8.7 58.2 %copy-start.9 = (f32[4096]{0:T(1024)S(1)}, f32[4096]{0:T(1024)}, u32[]{:S(2)}) copy-start(f32[4096]{0:T(1024)} %param.18) | copy-start | bytes 49156
  8.7 238.0 %all-gather.8.cloned.1.call-start = ((), (), s32[]{:S(2)}) async-start(), calls=%async_computation.2 | async-start | bytes 18874368 | tf_op jit(solution)/shard_map/all_gather | solution.py:433
  66.9 8.8 %copy-start.3 = (bf16[1024,32]{0,1:T(8,128)(2,1)S(1)}, bf16[1024,32]{0,1:T(8,128)(2,1)}, u32[]{:S(2)}) copy-start(bf16[1024,32]{0,1:T(8,128)(2,1)} %param.24) | copy-start | bytes 196612
  66.9 9.3 %copy-start.5 = (f32[1024]{0:T(1024)S(1)}, f32[1024]{0:T(1024)}, u32[]{:S(2)}) copy-start(f32[1024]{0:T(1024)} %param.22) | copy-start | bytes 12292
  72.7 3.3 %collective-permute-start = (bf16[2,3,1024]{2,1,0:T(4,128)(2,1)S(1)}, bf16[2,3,1024]{2,1,0:T(4,128)(2,1)S(1)}, u32[]{:S(2)}, u32[]{:S(2)}) collective-permute-start(bf16[2,3,1024]{2,1,0:T(4,128)(2,1)S(1)} %slice.40), channel_id=1, source_target_pairs={{0,4},{4,8},{8,12},{12,16},{16,20},{20,24},{24,28},{1,5},{5,9},{9,... | collective-permute-start | bytes 36872 | tf_op jit(solution)/shard_map/ppermute | solution.py:445
  76.2 1.1 copy-start.8
  76.9 17.8 %copy-start.2 = (f32[2,128,1024]{2,1,0:T(8,128)}, f32[2,128,1024]{2,1,0:T(8,128)S(1)}, u32[]{:S(2)}) copy-start(f32[2,128,1024]{2,1,0:T(8,128)S(1)} %divide_multiply_fusion) | copy-start | bytes 3145732
  242.5 4.2 %copy-start = (bf16[256,4096]{1,0:T(8,128)(2,1)S(1)}, bf16[256,4096]{1,0:T(8,128)(2,1)}, u32[]{:S(2)}) copy-start(bf16[256,4096]{1,0:T(8,128)(2,1)} %out_reduce.1) | copy-start | bytes 6291460
  242.5 4.2 %copy-start.10 = (f32[4096]{0:T(1024)S(1)}, f32[4096]{0:T(1024)}, u32[]{:S(2)}) copy-start(f32[4096]{0:T(1024)} %param.30) | copy-start | bytes 49156
Sparse Core Ops, SparseCore 0:
  9.9 56.9 all-gather.3
  68.8 57.0 all-gather.5
  127.8 96.5 all-gather.7

commit v2 on v1

--- a/solution.py
+++ b/solution.py
@@ -11,6 +11,9 @@
 VMEM = pl.BlockSpec(memory_space=pltpu.VMEM)
 CHUNKS = 8
 LANE = 128
+PIECES = 8
+LAG = 8
+LOG2E = 1.4426950408889634
 
 
 def peer(axis, shift):
@@ -133,6 +136,7 @@
                 rates = [
                     [
                         rate_ref[pl.ds(n, 1), pl.ds(pl.multiple_of((g * wide + w) * LANE, LANE), LANE)]
+                        * -LOG2E
                         for n in range(nstate)
                     ]
                     for w in range(wide)
@@ -155,7 +159,7 @@
                         for w in range(wide):
                             i = w * nstate + n
                             held[i] = (
-                                jnp.exp(-now[w] * rates[w][n]) * held[i] + push[w] * into
+                                jnp.exp2(now[w] * rates[w][n]) * held[i] + push[w] * into
                             )
                             if with_out:
                                 term = held[i] * outof
@@ -218,23 +222,30 @@
             for copy in pair(other, me):
                 copy.wait_recv()
 
-    @pl.loop(0, lanes)
-    def _(k):
-        cols = pl.ds(pl.multiple_of(k * LANE, LANE), LANE)
-        rate = rate_ref[:, cols]
-        for b in range(batch):
-            def earlier(d, carry):
-                decay = jnp.exp(-tot_in[d, pl.ds(b, 1), cols] * rate)
-                return decay * carry + agg_in[d, pl.ds(b * nstate, nstate), cols].astype(
-                    jnp.float32
-                )
-
-            carry = lax.fori_loop(0, me, earlier, jnp.zeros((nstate, LANE), jnp.float32))
+    group = 4 if lanes % 4 == 0 else 1
+
+    @pl.loop(0, lanes // group)
+    def _(g):
+        cols = [pl.ds(pl.multiple_of((g * group + w) * LANE, LANE), LANE) for w in range(group)]
+        rate = [rate_ref[:, at] for at in cols]
+        every = [(b, w) for b in range(batch) for w in range(group)]
+
+        def earlier(d, carry):
+            return tuple(
+                jnp.exp(-tot_in[d, pl.ds(b, 1), cols[w]] * rate[w]) * held
+                + agg_in[d, pl.ds(b * nstate, nstate), cols[w]].astype(jnp.float32)
+                for (b, w), held in zip(every, carry)
+            )
+
+        zero = jnp.zeros((nstate, LANE), jnp.float32)
+        starts = lax.fori_loop(0, me, earlier, (zero,) * len(every))
+        for (b, w), carry in zip(every, starts):
+            k = g * group + w
             for c in range(CHUNKS):
                 at = pl.ds(c, nstate, stride=CHUNKS)
                 part = state[b, k, at, :]
                 state[b, k, at, :] = carry
-                carry = jnp.exp(-sums[b, k, pl.ds(c, 1), :] * rate) * carry + part
+                carry = jnp.exp(-sums[b, k, pl.ds(c, 1), :] * rate[w]) * carry + part
 
     run(True)
 
@@ -272,83 +283,113 @@
     )(low, proj, bias, conv, rate)
 
 
-def out_kernel(nv, gated_ref, w_ref, resid_ref, out_ref, sent, recv, mine, s1, r1, s2, r2):
+def out_kernel(nv, gated_ref, w_ref, resid_ref, out_ref, mine, sent, recv, s1, r1, s2, r2):
     me = lax.axis_index("vocab")
     rows, width = resid_ref.shape
-    share = width // nv
-    greet(("vocab",))
-
-    def columns(index):
-        return pl.ds(pl.multiple_of(index * share, share), share)
-
-    tile = min(512, share)
-
-    def product(index, put):
-        @pl.loop(0, share // tile)
-        def _(k):
-            at = pl.multiple_of(index * share + k * tile, tile)
-            put(
-                pl.ds(pl.multiple_of(k * tile, tile), tile), pl.ds(at, tile),
-                jnp.dot(
-                    gated_ref[...], w_ref[:, pl.ds(at, tile)], preferred_element_type=jnp.float32
-                ),
-            )
-
-    copies = {}
-    order = sorted(range(1, nv), key=lambda s: abs(s - nv / 2))
-    for shift in order:
-        def put(local, whole, value):
-            sent[shift - 1, :, local] = value.astype(jnp.bfloat16)
-
-        product(lax.rem(me + shift, nv), put)
-        copy = remote(
-            sent.at[shift - 1], recv.at[shift - 1],
-            s1.at[shift - 1], r1.at[shift - 1], peer("vocab", shift),
-        )
-        copy.start()
-        copies[shift] = copy
-
-    def put(local, whole, value):
-        mine[:, local] = value
-
-    product(me, put)
-    for shift in order:
-        copies[shift].wait()
-
-    @pl.loop(0, share // tile)
+    half = width // 2
+    block = rows // PIECES
+    right = {"vocab": lax.rem(me + 1, nv)}
+    left = {"vocab": lax.rem(me + nv - 1, nv)}
+    barrier = pltpu.get_barrier_semaphore()
+
+    for place, device in ((me < nv - 1, right), (me > 0, left)):
+        @pl.when(place)
+        def _():
+            pl.semaphore_signal(barrier, inc=1, device_id=device, device_id_type=MESH)
+
+    tile = min(512, half)
+
+    @pl.loop(0, width // tile)
     def _(k):
-        local = pl.ds(pl.multiple_of(k * tile, tile), tile)
-        whole = pl.ds(pl.multiple_of(me * share + k * tile, tile), tile)
-        total = mine[:, local]
-        for shift in range(1, nv):
-            total = total + recv[shift - 1, :, local].astype(jnp.float32)
-        hidden = (resid_ref[:, whole].astype(jnp.float32) + total).astype(jnp.bfloat16)
-        sent[nv - 1, :, local] = hidden
-        out_ref[:, whole] = hidden
-
-    copies = []
-    for shift in range(1, nv):
-        copy = remote(
-            sent.at[nv - 1], out_ref.at[:, columns(me)],
-            s2.at[shift - 1], r2.at[shift - 1], peer("vocab", shift),
-        )
-        copy.start()
-        copies.append(copy)
-    for copy in copies:
-        copy.wait()
+        cols = pl.ds(pl.multiple_of(k * tile, tile), tile)
+        mine[:, cols] = jnp.dot(
+            gated_ref[...], w_ref[:, cols], preferred_element_type=jnp.float32
+        )
+
+    at_end = jnp.logical_or(me == 0, me == nv - 1)
+
+    @pl.when(at_end)
+    def _():
+        pl.semaphore_wait(barrier, 1)
+
+    @pl.when(jnp.logical_not(at_end))
+    def _():
+        pl.semaphore_wait(barrier, 2)
+
+    ways = ((me, right, left), (nv - 1 - me, left, right))
+
+    def up_copy(h, c):
+        at = pl.ds(c * block, block)
+        return remote(
+            sent.at[h, at], recv.at[h, at], s1.at[h, c], r1.at[h, c], ways[h][1]
+        )
+
+    def down_copy(h, c):
+        view = out_ref.at[pl.ds(c * block, block), pl.ds(h * half, half)]
+        return remote(view, view, s2.at[h, c], r2.at[h, c], ways[h][2])
+
+    def up(h, c):
+        place = ways[h][0]
+        at = pl.ds(c * block, block)
+        cols = pl.ds(h * half, half)
+
+        @pl.when(place > 0)
+        def _():
+            up_copy(h, c).wait_recv()
+            mine[at, cols] = mine[at, cols] + recv[h, at, :].astype(jnp.float32)
+
+        @pl.when(place < nv - 1)
+        def _():
+            sent[h, at, :] = mine[at, cols].astype(jnp.bfloat16)
+            up_copy(h, c).start()
+
+        @pl.when(place == nv - 1)
+        def _():
+            out_ref[at, cols] = (
+                resid_ref[at, cols].astype(jnp.float32) + mine[at, cols]
+            ).astype(jnp.bfloat16)
+            down_copy(h, c).start()
+
+    def down(h, c):
+        place = ways[h][0]
+
+        @pl.when(place < nv - 1)
+        def _():
+            down_copy(h, c).wait_recv()
+
+            @pl.when(place > 0)
+            def _():
+                down_copy(h, c).start()
+
+    for step in range(PIECES + LAG):
+        if step < PIECES:
+            up(0, step)
+            up(1, step)
+        if step >= LAG:
+            down(0, step - LAG)
+            down(1, step - LAG)
+    for h in range(2):
+        place = ways[h][0]
+        for c in range(PIECES):
+            @pl.when(place < nv - 1)
+            def _():
+                up_copy(h, c).wait_send()
+
+            @pl.when(place > 0)
+            def _():
+                down_copy(h, c).wait_send()
 
 
 def out_reduce(gated, w, resid, nv):
     rows, width = resid.shape
-    share = width // nv
-    sems = [pltpu.SemaphoreType.DMA((nv - 1,))] * 4
+    sems = [pltpu.SemaphoreType.DMA((2, PIECES))] * 4
     return call(
         functools.partial(out_kernel, nv),
         jax.ShapeDtypeStruct((rows, width), jnp.bfloat16),
         [
-            pltpu.VMEM((nv, rows, share), jnp.bfloat16),
-            pltpu.VMEM((nv - 1, rows, share), jnp.bfloat16),
-            pltpu.VMEM((rows, share), jnp.float32),
+            pltpu.VMEM((rows, width), jnp.float32),
+            pltpu.VMEM((2, rows, width // 2), jnp.bfloat16),
+            pltpu.VMEM((2, rows, width // 2), jnp.bfloat16),
         ] + sems,
         3, 60, "out_reduce",
     )(gated, w, resid)

time: 294 us -> 485 us (1.65)
  Pallas kernels: 180 us -> 371 us
    pallas_call x1, Pallas kernels: 102 us -> 293 us  [out_reduce(): call(functools.partial(out_kernel, nv), jax.ShapeDtypeStruct((rows, width...]
  transfers between devices with their start and end apart: 4 -> 4, of which waited for: 1 -> 1; matrix products, arithmetic and copies ran while one was open for 7% -> 4% of each run, Pallas kernels for 53% -> 72%
where the time goes in v2:
time: 485 us
  Pallas kernels  371 us (76%)
  waiting for transfers between devices  58.3 us (12%)
  matrix products  23.6 us (5%)
  between operations  16.4 us (3%)
  other arithmetic  7.55 us (2%)
  local copies, waits for them, and re-layouts  5.26 us (1%)
    pallas_call x1, Pallas kernels, out_reduce(): call(functools.partial(out_kernel, nv), jax.ShapeDtypeStruct((rows, width...  293 us
    all_gather x1, waiting for transfers between devices, body(): full_x = lax.all_gather(in_x, 'dp', axis=0, tiled=True)  56.2 us
    pallas_call x1, Pallas kernels, scan(): call(functools.partial(scan_kernel, nd, batch, nstate, ranks), jax.ShapeD...  39.1 us
    pallas_call x1, Pallas kernels, tail(): call(functools.partial(tail_kernel, nv, nd), (jax.ShapeDtypeStruct((1, ro...  22.9 us
    pallas_call x1, Pallas kernels, dt_reduce(): call(functools.partial(dt_kernel, nv, ranks), jax.ShapeDtypeStruct((rows,...  16.3 us
  transfers between devices with their start and end apart: 4, of which 1 were waited for; matrix products, arithmetic and copies ran while one was open for 4% of the time, Pallas kernels for 72%

profile of v2, /device:TPU:0, one launch (start us, length us, event | category | flops | bytes accessed | tf_op | source)
XLA Modules:
  0.0 484.9 jit_solution(13598839506406619055)
XLA Ops:
  7.2 0.0 all-gather.4.cloned.1.call-start
  7.2 0.7 all-gather.4.cloned.1.call-update
  7.9 0.0 all-gather.6.cloned.1.call-start
  8.0 0.7 all-gather.6.cloned.1.call-update
  8.7 0.0 all-gather.8.cloned.1.call-start
  8.7 0.7 all-gather.8.cloned.1.call-update
  9.5 0.5 multiply_reduce_fusion
  10.0 0.6 compare_convert_fusion
  10.7 56.2 %all-gather.4.cloned.1.call-done = bf16[4096,1024]{1,0:T(8,128)(2,1)} async-done(((bf16[512,1024]{1,0:T(8,128)(2,1)}), bf16[4096,1024]{1,0:T(8,128)(2,1)}) %all-gather.4.cloned.1.call-update) | async-done | bytes 8388624 | tf_op jit(solution)/shard_map/all_gather | solution.py:471
  66.9 5.8 %convolution_convert_fusion.1 = bf16[256,1024]{1,0:T(8,128)(2,1)S(1)} fusion(bf16[4096,1024]{1,0:T(8,128)(2,1)} %all-gather.4.cloned.1.call-done, bf16[256,4096]{1,0:T(8,128)(2,1)S(1)} %bitcast.25, f32[4096]{0:T(1024)S(1)} %copy-done.9, f32[256]{0:T(256)S(1)} %rsqrt_bitcast_fusion), kind=kOutput, calls=%fused_computation.16 | convolution fusion | flops 2151940096 | bytes 11027456 | tf_op jit(solution)/shard_map/dot_general | solution.py:482
  72.7 2.2 collective-permute-start
  74.9 0.6 convert_reduce_fusion
  75.5 0.2 copy.20
  75.7 0.1 pad.6.clone
  75.8 0.1 pad.3.clone
  75.8 0.1 maximum_convert_fusion
  76.0 0.7 divide_multiply_fusion
  76.7 0.4 copy-done.8
  77.1 1.1 convolution_convert_fusion.2.part_ref
  78.2 16.3 %dt_reduce.1.low_ref = bf16[256,384]{1,0:T(8,128)(2,1)} custom-call(bf16[256,384]{1,0:T(8,128)(2,1)} %convolution_convert_fusion.2.part_ref, f32[1,256]{1,0:T(1,128)} %bitcast.42), custom_call_target="tpu_custom_call" | custom-call | bytes 30000000 | tf_op jit(solution)/shard_map/dt_reduce/pallas_call | solution.py:93
  94.5 39.1 %scan.1 = f32[256,1024]{1,0:T(8,128)} custom-call(bf16[256,384]{1,0:T(8,128)(2,1)} %dt_reduce.1.low_ref, bf16[256,1024]{1,0:T(8,128)(2,1)} %proj_ref.1, f32[1,1024]{1,0:T(1,128)} %bitcast.37, f32[256,1024]{1,0:T(8,128)} %bitcast.28, f32[16,1024]{1,0:T(8,128)} %bitcast.32), custom_call_target="tpu_custom_call" | custom-call | bytes 90000000 | tf_op jit(solution)/shard_map/scan/pallas_call | solution.py:268
  133.6 0.0 all-gather.6.cloned.1.call-done
  133.7 7.0 %fusion.11.gated_ref = bf16[256,1024]{1,0:T(8,128)(2,1)} fusion(f32[256,1024]{1,0:T(8,128)} %scan.1, bf16[4096,1024]{1,0:T(8,128)(2,1)} %all-gather.6.cloned.1.call-done, bf16[256,4096]{1,0:T(8,128)(2,1)S(1)} %bitcast.26, f32[4096]{0:T(1024)S(1)} %copy-done.9, f32[256]{0:T(256)S(1)} %rsqrt_bitcast_fusion), kind=kOutput, calls=%fused_computation.22 | convolution fusion | flops 2153775104 | bytes 12076032 | tf_op jit(solution)/shard_map/dot_general | solution.py:500
  140.6 293.2 %out_reduce.1 = bf16[256,4096]{1,0:T(8,128)(2,1)} custom-call(bf16[256,1024]{1,0:T(8,128)(2,1)} %fusion.11.gated_ref, bf16[1024,4096]{1,0:T(8,128)(2,1)} %w_ref.1, bf16[256,4096]{1,0:T(8,128)(2,1)} %bitcast.24), custom_call_target="tpu_custom_call" | custom-call | bytes 180000000 | tf_op jit(solution)/shard_map/out_reduce/pallas_call | solution.py:386
  433.9 2.0 constant_dynamic-slice_fusion
  435.9 2.1 fusion
  438.1 9.7 %fusion.24 = (f32[256]{0:T(256)S(1)}, f32[256,2048]{1,0:T(8,128)}) fusion(bf16[2048,4096]{1,0:T(8,128)(2,1)} %all-gather.8.cloned.1.call-done, bf16[256,4096]{1,0:T(8,128)(2,1)S(1)} %copy-done, f32[4096]{0:T(1024)S(1)} %copy-done.10, f32[256]{0:T(256)S(1)} %add_rsqrt_fusion), kind=kOutput, calls=%fused_computation.49 | convolution fusion | flops 4299685888 | bytes 20989952 | tf_op jit(solution)/shard_map/dot_general | solution.py:509
  447.8 2.2 exponential_reduce_fusion
  450.0 0.7 maximum_maximum_fusion.stats_ref
  450.6 22.9 %tail.1 = (f32[1,256]{1,0:T(1,128)}, f32[8,128]{1,0:T(8,128)}) custom-call(f32[8,256]{1,0:T(8,128)} %maximum_maximum_fusion.stats_ref, f32[1,256]{1,0:T(1,128)} %bitcast.41), custom_call_target="tpu_custom_call" | custom-call | bytes 18000000 | tf_op jit(solution)/shard_map/tail/pallas_call | solution.py:439
  473.5 1.2 slice.39
  476.0 1.2 copy.22
  (31 shorter events, 0.1 us)
Async XLA Ops:
  7.2 2.3 copy-start.1
  7.2 59.7 %all-gather.4.cloned.1.call-start = ((), (), s32[]{:S(2)}) async-start(), calls=%async_computation | async-start | bytes 9437184 | tf_op jit(solution)/shard_map/all_gather | solution.py:471
  7.9 125.8 %all-gather.6.cloned.1.call-start = ((), (), s32[]{:S(2)}) async-start(), calls=%async_computation.1 | async-start | bytes 9437184 | tf_op jit(solution)/shard_map/all_gather | solution.py:473
  8.7 1.3 copy-start.6
  8.7 1.3 copy-start.7
  8.7 2.0 copy-start.4
  8.7 58.2 %copy-start.9 = (f32[4096]{0:T(1024)S(1)}, f32[4096]{0:T(1024)}, u32[]{:S(2)}) copy-start(f32[4096]{0:T(1024)} %param.18) | copy-start | bytes 49156
  8.7 429.3 %all-gather.8.cloned.1.call-start = ((), (), s32[]{:S(2)}) async-start(), calls=%async_computation.2 | async-start | bytes 18874368 | tf_op jit(solution)/shard_map/all_gather | solution.py:474
  66.9 8.6 %copy-start.3 = (bf16[1024,32]{0,1:T(8,128)(2,1)S(1)}, bf16[1024,32]{0,1:T(8,128)(2,1)}, u32[]{:S(2)}) copy-start(bf16[1024,32]{0,1:T(8,128)(2,1)} %param.24) | copy-start | bytes 196612
  66.9 9.1 %copy-start.5 = (f32[1024]{0:T(1024)S(1)}, f32[1024]{0:T(1024)}, u32[]{:S(2)}) copy-start(f32[1024]{0:T(1024)} %param.22) | copy-start | bytes 12292
  72.7 3.1 collective-permute-start
  76.0 1.1 copy-start.8
  76.7 17.9 %copy-start.2 = (f32[2,128,1024]{2,1,0:T(8,128)}, f32[2,128,1024]{2,1,0:T(8,128)S(1)}, u32[]{:S(2)}) copy-start(f32[2,128,1024]{2,1,0:T(8,128)S(1)} %divide_multiply_fusion) | copy-start | bytes 3145732
  433.9 4.2 copy-start
  433.9 4.2 copy-start.10
Sparse Core Ops, SparseCore 0:
  9.9 56.9 all-gather.3
  68.8 57.0 all-gather.5
  127.8 96.1 all-gather.7
